TPU v7x, 128 devices: a whole 4x4x4 slice. The times are simulated.
128 devices in a mesh: grp: 8 (over y_hi, z), pair: 16 (over x, y_lo, core).
Axes of the slice: x: 4, y: 4 (y_hi: 2, y_lo: 2; y = y_hi * 2 + y_lo), z: 4, core: 2. Of those that a mesh axis runs over, the one named last changes fastest.
Arguments:
- amplitudes: bfloat16 [128, 512, 512], P('pair', 'grp'), may hold values from -6 to 6
- cholesky: bfloat16 [512, 512, 2048], P('pair', 'grp'), may hold values from -0.09375 to 0.09375
Outputs:
- ladder_term: float32 [512, 4, 128], P('pair', None, 'grp')
All inputs are finite; a program needn't handle non-finite values.
Results may differ from a plain program's by a relative error of at most 0.003.
Values may be sent and summed in bfloat16 or wider, within the bound.
A program may use at most 128 MiB of HBM per device.

v0:
```python
import jax
import jax.numpy as jnp
from jax import lax
from jax.sharding import PartitionSpec as P

A_WIN = 4


def from_root(x, axis, root):
    return lax.dynamic_index_in_dim(lax.all_gather(x, axis), root, 0, keepdims=False)


def split_up(x, dim, length):
    before, after = (x.shape[:dim], x.shape[dim + 1 :])
    return jnp.moveaxis(x.reshape(*before, length, -1, *after), dim, 0)


def sent_and_summed(x, axis, dim):
    length = lax.axis_size(axis)
    blocks = lax.all_to_all(split_up(x, dim, length), axis, 0, 0, tiled=True)
    return jnp.sum(blocks, axis=0)


def build_tile(chol_local, portion):
    return lax.dot_general(
        chol_local, portion, (((2,), (2,)), ((), ())), preferred_element_type=jnp.float32
    ).astype(jnp.bfloat16)


def ladder(integrals, amp_part):
    return lax.dot_general(
        integrals, amp_part, (((1, 3), (1, 2)), ((), ())), preferred_element_type=jnp.float32
    )


def per_device(amplitudes, cholesky):
    own_window = cholesky[:A_WIN]
    everyone = lax.all_gather(amplitudes, "pair", axis=0, tiled=True)
    shared = from_root(own_window, "pair", 0)
    summed = ladder(
        build_tile(cholesky, lax.all_gather(shared, "grp", axis=1, tiled=True)), everyone
    )
    return sent_and_summed(summed, "grp", 2)


def solution(mesh):
    in_specs = (P("pair", "grp", None), P("pair", "grp", None))
    out_specs = P("pair", None, "grp")
    return jax.shard_map(
        per_device, mesh=mesh, in_specs=in_specs, out_specs=out_specs, check_vma=False
    )
```

profile of v0, /device:TPU:5, one launch (start us, length us, event | category | flops | bytes accessed | tf_op | source)
XLA Modules:
  0.0 332.1 jit_solution(7351327069050586795)
XLA Ops:
  6.5 0.0 all-gather.9.cloned.1.call-start
  6.5 2.4 slice.4
  8.9 0.0 all-gather.9.cloned.1.call-update
  8.9 0.0 all-gather.7.cloned.1.call-start
  9.0 2.1 copy.7
  11.1 0.0 all-gather.7.cloned.1.call-update
  11.1 0.0 all-gather.11.cloned.1.call-start
  11.2 91.7 %all-gather.9.cloned.1.call-done = bf16[64,64,2048]{2,1,0:T(8,128)(2,1)} async-done(((bf16[4,64,2048]{2,1,0:T(8,128)(2,1)}), bf16[64,64,2048]{2,1,0:T(8,128)(2,1)}) %all-gather.9.cloned.1.call-update) | async-done | bytes 16777232 | tf_op jit(solution)/shard_map/all_gather | solution.py:10
  102.9 2.4 slice.6
  105.3 0.0 all-gather.11.cloned.1.call-update
  105.3 52.2 %all-gather.7.cloned.1.call-done = bf16[128,64,512]{2,0,1:T(8,128)(2,1)} async-done(((bf16[8,64,512]{2,0,1:T(8,128)(2,1)}), bf16[128,64,512]{2,0,1:T(8,128)(2,1)}) %all-gather.7.cloned.1.call-update) | async-done | bytes 8388624 | tf_op jit(solution)/shard_map/all_gather | solution.py:38
  157.5 109.2 %all-gather.11.cloned.1.call-done = bf16[4,512,2048]{2,1,0:T(8,128)(2,1)} async-done(((bf16[4,64,2048]{2,1,0:T(8,128)(2,1)}), bf16[4,512,2048]{2,1,0:T(8,128)(2,1)}) %all-gather.11.cloned.1.call-update) | async-done | bytes 8388624 | tf_op jit(solution)/shard_map/all_gather | solution.py:41
  266.7 47.5 %fusion.2 = f32[32,4,128,1]{0,2,3,1:T(8,128)S(1)} fusion(bf16[128,64,512]{2,0,1:T(8,128)(2,1)} %all-gather.7.cloned.1.call-done, bf16[4,512,2048]{2,1,0:T(8,128)(2,1)} %all-gather.11.cloned.1.call-done, bf16[32,64,2048]{2,1,0:T(8,128)(2,1)} %param.3), kind=kOutput, calls=%fused_computation.2 | convolution fusion | flops 18257805312 | bytes 25231360 | tf_op jit(solution)/shard_map/dot_general | solution.py:31
  314.2 0.2 reshape.13
  314.4 9.1 %all_to_all.5 = f32[8,1,2048]{2,1,0:T(1,128)S(1)} all-to-all(f32[8,1,2048]{2,1,0:T(1,128)S(1)} %reshape.13), channel_id=1, replica_groups=mesh['grp'=8,'pair'=16] {'grp'}, dimensions={0} | all-to-all | bytes 131072 | tf_op jit(solution)/shard_map/all_to_all | solution.py:20
  323.5 0.5 broadcast
  324.0 0.8 reduce
  324.8 0.1 reshape.14
  324.9 0.6 bitcast_reduce_fusion
  (1 shorter events, 0.0 us)
Async XLA Ops:
  6.5 96.3 %all-gather.9.cloned.1.call-start = ((), (), s32[]{:S(2)}) async-start(), calls=%async_computation.2 | async-start | bytes 17825792 | tf_op jit(solution)/shard_map/all_gather | solution.py:10
  8.9 148.5 %all-gather.7.cloned.1.call-start = ((), (), s32[]{:S(2)}) async-start(), calls=%async_computation.1 | async-start | bytes 8912896 | tf_op jit(solution)/shard_map/all_gather | solution.py:38
  11.1 255.6 %all-gather.11.cloned.1.call-start = ((), (), s32[]{:S(2)}) async-start(), calls=%async_computation.3 | async-start | bytes 9437184 | tf_op jit(solution)/shard_map/all_gather | solution.py:41
Sparse Core Ops, SparseCore 0:
  9.1 93.7 all-gather.8
  104.5 52.8 all-gather.6
  159.8 106.8 all-gather.10
where the time goes:
time: 335 us; the launch traced here: 332 us
  waiting for transfers between devices  253 us (76%)
  matrix products  47.5 us (14%)
  between operations  13.1 us (4%)
  blocking collectives  9.08 us (3%)
  local copies, waits for them, and re-layouts  7.68 us (2%)
    all_gather x1, waiting for transfers between devices, per_device(): lax.all_gather(shared, 'grp', axis=1, tiled=True)  109 us
    all_gather x1, waiting for transfers between devices, from_root(): lax.all_gather(x, axis)  91.7 us
    all_gather x1, waiting for transfers between devices, per_device(): everyone = lax.all_gather(amplitudes, 'pair', axis=0, tiled=True)  52.2 us
    dot_general x1, matrix products, ladder(): lax.dot_general(integrals, amp_part, (((1, 3), (1, 2)), ((), ())), prefer...  47.5 us
    all_to_all x1, blocking collectives, sent_and_summed(): blocks = lax.all_to_all(split_up(x, dim, length), axis, 0, 0, tiled=True)  9.08 us
  transfers between devices with their start and end apart: 3, of which 3 were waited for; matrix products, arithmetic and copies ran while one was open for 1% of the time, Pallas kernels for 0%

commit v1 on v0

v1 whole, which is shorter than its diff:
```python
import jax
import jax.numpy as jnp
from jax import lax
from jax.experimental import pallas as pl
from jax.experimental.pallas import tpu as pltpu
from jax.sharding import PartitionSpec as P

A_WIN = 4
MESH = pl.DeviceIdType.MESH
F32, BF16 = jnp.float32, jnp.bfloat16


ROW_CHUNK = 1024
X_OF_PIECE = (0, 1, 0, 3)
ROW_PLAN = (
    ((0, (1, 0)), (2, (1, 0)), (1, (0,)), (3, (1,))),
    ((1, (0, 1)), (0, (1,)), (2, ()), (3, ())),
    ((0, ()), (1, ()), (2, ()), (3, ())),
    ((3, (1, 0)), (2, (0,)), (0, ()), (1, ())),
)


def kernel(
    amp, chol_t, chol, out,
    rows_l, win, amps, ints, total, turned, parts,
    loc_sem, t_sem, w_sem, p_sem, l_sem, r_sem, s_sem,
):
    g, p = lax.axis_index("grp"), lax.axis_index("pair")
    x, y_lo, h = p // 4, (p // 2) % 2, p % 2
    y_hi, z = g // 4, g % 4
    y = 2 * y_hi + y_lo
    xr, xl = (x + 1) % 4, (x + 3) % 4
    zu, zd, zf = (z + 1) % 4, (z + 3) % 4, (z + 2) % 4
    y_l = 2 * y_hi + (1 - y_lo)
    y_h = 2 * (1 - y_hi) + (1 - y_lo)
    y_f = 2 * (1 - y_hi) + y_lo

    def dev(xx, yy, zz, hh):
        return ((yy // 2) * 4 + zz, xx * 4 + (yy % 2) * 2 + hh)

    sib = dev(x, y, z, 1 - h)
    right, left = dev(xr, y, z, h), dev(xl, y, z, h)
    lo, hi = dev(x, y_l, z, h), dev(x, y_h, z, h)
    up, down = dev(x, y, zu, h), dev(x, y, zd, h)

    started = []
    n_sent = [0]

    def remote(src, dst, recv, to, k):
        return pltpu.make_async_remote_copy(
            src_ref=src, dst_ref=dst, send_sem=s_sem.at[k], recv_sem=recv, device_id=to, device_id_type=MESH
        )

    def send(src, dst, recv, to):
        c = remote(src, dst, recv, to, n_sent[0])
        n_sent[0] += 1
        c.start()
        started.append(c)

    def arrived(dst, recv):
        remote(dst, dst, recv, sib, 0).wait_recv()

    def blk(i):
        return amps.at[i]

    def wblk(a, zz):
        return win.at[zz // 2, a, zz % 2]

    def piece(a, zz, j):
        return win.at[zz // 2, a, zz % 2, pl.ds(16 * j, 16)]

    def send_t(i, to):
        send(blk(i), blk(i), t_sem.at[i], to)

    def send_w(a, zz, to):
        send(wblk(a, zz), wblk(a, zz), w_sem.at[a * 4 + zz], to)

    def wait_t(i):
        arrived(blk(i), t_sem.at[i])

    def wait_w(a, zz):
        arrived(wblk(a, zz), w_sem.at[a * 4 + zz])

    half = pl.ds(pl.multiple_of(h * 256, 256), 256)
    other = pl.ds(pl.multiple_of((1 - h) * 256, 256), 256)
    own_t = pltpu.make_async_copy(amp.at[:, :, half], blk(p), loc_sem.at[0])
    own_t.start()
    own_l = pltpu.make_async_copy(chol_t, rows_l.at[h], loc_sem.at[1])
    own_l.start()

    barrier = pltpu.get_barrier_semaphore()

    def hello(to):
        pl.semaphore_signal(barrier, inc=1, device_id=to, device_id_type=MESH)

    me = g * 2 + h

    def peer(o):
        i = (me + o) % 16
        return i // 2, (p // 2) * 2 + i % 2, i

    for to in (right, left, lo, hi):
        hello(to)
    for o in range(1, 16):
        hello(peer(o)[:2])
    is_source = p == 0

    @pl.when((x != 2) & jnp.logical_not(is_source & (g < 4)))
    def _():
        hello((h * 4 + z, 0))

    @pl.when(jnp.logical_not(is_source))
    def _():
        pl.semaphore_wait(barrier, 19)

    @pl.when(is_source & (y_hi == 0))
    def _():
        pl.semaphore_wait(barrier, 30)

    @pl.when(is_source & (y_hi == 1))
    def _():
        pl.semaphore_wait(barrier, 31)

    n_scatter = n_sent[0]

    def scatter(top):
        k = n_scatter
        for qy in ((2 * top + 2) % 4, (2 * top + 1) % 4, (2 * top + 3) % 4, 2 * top):
            for j in (1, 3, 0, 2):
                src, dst = chol.at[qy, pl.ds(16 * j, 16)], piece(qy, z, j)
                if top == 0 and qy == 0 and X_OF_PIECE[j] == 0:
                    yield None, pltpu.make_async_copy(src, dst, p_sem.at[j])
                else:
                    yield remote(src, dst, p_sem.at[j], dev(X_OF_PIECE[j], qy, z, top), k), None
                    k += 1

    for top in (0, 1):

        @pl.when(is_source & (y_hi == top))
        def _():
            for away, here in scatter(top):
                (away or here).start()

    n_sent[0] = n_scatter + 16

    send(amp.at[:, :, other], blk(p), t_sem.at[p], sib)
    own_t.wait()
    for to in (right, left, lo):
        send_t(p, to)
    send(chol_t, rows_l.at[h], l_sem, sib)

    n_row = n_sent[0]

    def got(j):
        arrived(piece(y, z, j), p_sem.at[j])

    def row(xx):
        k = n_row
        for j, tos in ROW_PLAN[xx]:
            copies = []
            for to in tos:
                copies.append(remote(piece(y, z, j), piece(y, z, j), p_sem.at[j], (left, right)[to], k))
                k += 1
            yield j, copies

    for xx in range(4):

        @pl.when(x == xx)
        def _():
            for j, copies in row(xx):
                got(j)
                for c in copies:
                    c.start()

    n_sent[0] = n_row + 6

    for to in (down, up, hi, lo):
        send_w(y, z, to)
    sib_p = (p // 2) * 2 + (1 - h)
    wait_t(sib_p)
    for to in (right, left, lo):
        send_t(sib_p, to)
    wait_w(y_l, z)
    for to in (down, up, hi):
        send_w(y_l, z, to)
    lo_p = x * 4 + (1 - y_lo) * 2 + h
    lo_s = x * 4 + (1 - y_lo) * 2 + (1 - h)
    wait_t(lo_p)
    for to in (right, left):
        send_t(lo_p, to)
    wait_w(y, zd)
    send_w(y, zd, hi)
    wait_w(y, zu)
    send_w(y, zu, hi)
    send_w(y, zu, down)
    wait_w(y_f, z)
    for to in (down, up):
        send_w(y_f, z, to)
    fr = xl * 4 + y_lo * 2
    fl = xr * 4 + (1 - y_lo) * 2
    wait_t(fr + h)
    send_t(fr + h, right)
    wait_t(lo_s)
    for to in (right, left):
        send_t(lo_s, to)
    wait_t(fl + h)
    send_t(fl + h, left)
    wait_t(fr + (1 - h))
    send_t(fr + (1 - h), right)

    wait_w(y_l, zd)
    send_w(y_l, zd, up)
    wait_w(y_l, zu)

    own_l.wait()
    arrived(rows_l.at[1 - h], l_sem)

    wide = ROW_CHUNK // 32

    def tile(zz, aa):
        w = win[zz, pl.ds(2 * aa, 2)].reshape(256, 2048)
        lanes = pl.ds(pl.multiple_of(zz * 128, 128), 128)

        def body(i, carry):
            k, d0 = i // (64 // wide), (i % (64 // wide)) * wide
            l = rows_l[k, pl.ds(d0, wide)].reshape(ROW_CHUNK, 2048)
            o = lax.dot_general(l, w, (((1,), (1,)), ((), ())), preferred_element_type=F32).astype(BF16)
            for q in (0, 1):
                ints[pl.ds(d0, wide), k * 4 + 2 * aa + q, :, lanes] = o[:, q * 128 : q * 128 + 128].reshape(
                    wide, 32, 128
                )
            return carry

        lax.fori_loop(0, 2 * (64 // wide), body, 0)

    zz, aa = z // 2, y // 2
    tile(zz, aa)

    wait_t(fl + (1 - h))
    send_t(fl + (1 - h), left)
    wait_w(y_h, zd)
    send_w(y_h, zd, up)
    wait_w(y_f, zu)
    send_w(y_f, zu, down)
    wait_w(y_h, zu)
    wait_w(y_h, z)
    wait_w(y_f, zd)
    tile(zz, 1 - aa)
    wait_w(y, zf)
    wait_w(y_l, zf)
    tile(1 - zz, aa)
    wait_w(y_f, zf)
    wait_w(y_h, zf)
    tile(1 - zz, 1 - aa)

    for k in (0, 1):
        wait_t(xr * 4 + y_lo * 2 + k)
        wait_t(xl * 4 + (1 - y_lo) * 2 + k)
    for k in range(4):
        wait_t(((x + 2) % 4) * 4 + k)

    total[...] = jnp.zeros_like(total)

    def step(i, carry):
        acc = None
        for u in range(4):
            d = i * 4 + u
            o = lax.dot_general(
                ints[d].reshape(256, 256), amps[:, d].reshape(128, 256), (((1,), (1,)), ((), ())),
                preferred_element_type=F32,
            )
            acc = o if acc is None else acc + o
        total[...] += acc
        return carry

    lax.fori_loop(0, 16, step, 0)
    turned[...] = total[...].T

    for o in range(1, 16):
        gg, pp, i = peer(o)
        send(
            turned.at[pl.ds(pl.multiple_of(gg * 16, 16), 16), pl.ds(pl.multiple_of((i % 2) * 128, 128), 128)],
            parts.at[me], r_sem.at[me], (gg, pp),
        )
    acc = turned[pl.ds(pl.multiple_of(g * 16, 16), 16), pl.ds(pl.multiple_of(h * 128, 128), 128)]
    for o in range(1, 16):
        i = peer(o)[2]
        arrived(parts.at[i], r_sem.at[i])
        acc = acc + parts[i]
    for a in range(A_WIN):
        out[a] = acc[:, a * 32 : a * 32 + 32]

    for c in started:
        c.wait_send()
    for top in (0, 1):

        @pl.when(is_source & (y_hi == top))
        def _():
            for away, _ in scatter(top):
                if away is not None:
                    away.wait_send()

    for xx in (0, 1, 3):

        @pl.when(x == xx)
        def _():
            for _, copies in row(xx):
                for c in copies:
                    c.wait_send()


def per_device(amplitudes, cholesky):
    hbm = pl.BlockSpec(memory_space=pltpu.MemorySpace.HBM)
    out = pl.pallas_call(
        kernel,
        out_shape=jax.ShapeDtypeStruct((A_WIN, 16, 32), F32),
        in_specs=[hbm] * 3,
        out_specs=pl.BlockSpec(memory_space=pltpu.VMEM),
        scratch_shapes=[
            pltpu.VMEM((2, 64, 32, 2048), BF16),
            pltpu.VMEM((2, A_WIN, 2, 64, 2048), BF16),
            pltpu.VMEM((16, 64, 8, 256), BF16),
            pltpu.VMEM((64, 8, 32, 256), BF16),
            pltpu.VMEM((256, 128), F32),
            pltpu.VMEM((128, 256), F32),
            pltpu.VMEM((16, 16, 128), F32),
            pltpu.SemaphoreType.DMA((2,)),
            pltpu.SemaphoreType.DMA((16,)),
            pltpu.SemaphoreType.DMA((16,)),
            pltpu.SemaphoreType.DMA((4,)),
            pltpu.SemaphoreType.DMA,
            pltpu.SemaphoreType.DMA((16,)),
            pltpu.SemaphoreType.DMA((80,)),
        ],
        compiler_params=pltpu.CompilerParams(
            collective_id=0, has_side_effects=True, vmem_limit_bytes=56 * 2**20
        ),
    )(amplitudes.transpose(1, 0, 2), cholesky.transpose(1, 0, 2), cholesky)
    return out.transpose(2, 0, 1)


def solution(mesh):
    in_specs = (P("pair", "grp", None), P("pair", "grp", None))
    out_specs = P("pair", None, "grp")
    return jax.shard_map(
        per_device, mesh=mesh, in_specs=in_specs, out_specs=out_specs, check_vma=False
    )
```

time: 335 us -> 89.3 us (0.27)
  waiting for transfers between devices: 253 us -> 0 us
  Pallas kernels: 0 us -> 73.2 us
  matrix products: 47.5 us -> 0 us
  between operations: 13.1 us -> 0.01 us
  blocking collectives: 9.08 us -> 0 us
  local copies, waits for them, and re-layouts: 7.68 us -> 14.8 us
    all_gather x3 -> x0, waiting for transfers between devices: 253 us -> none  [the longest x1 109 us: per_device(): lax.all_gather(shared, 'grp', axis=1, tiled=True)]
    pallas_call x0 -> x1, Pallas kernels: none -> 73.2 us  [per_device(): pl.pallas_call(kernel, out_shape=jax.ShapeDtypeStruct((A_WIN, 16, 32), F3...]
    dot_general x1 -> x0, matrix products: 47.5 us -> none  [ladder(): lax.dot_general(integrals, amp_part, (((1, 3), (1, 2)), ((), ())), prefer...]
    unnamed x3, local copies, waits for them, and re-layouts: 2.39 us -> 14.8 us
    all_to_all x1 -> x0, blocking collectives: 9.08 us -> none  [sent_and_summed(): blocks = lax.all_to_all(split_up(x, dim, length), axis, 0, 0, tiled=True)]
  transfers between devices with their start and end apart: 3 -> 0, of which waited for: 3 -> 0; matrix products, arithmetic and copies ran while one was open for 1% -> 0% of each run, Pallas kernels for 0% -> 0%
where the time goes in v1:
time: 89.3 us; the launch traced here: 88 us
  Pallas kernels  73.2 us (82%)
  local copies, waits for them, and re-layouts  14.8 us (17%)
    pallas_call x1, Pallas kernels, per_device(): pl.pallas_call(kernel, out_shape=jax.ShapeDtypeStruct((A_WIN, 16, 32), F3...  73.2 us
    unnamed x3, local copies, waits for them, and re-layouts  14.8 us

profile of v1, /device:TPU:5, one launch (start us, length us, event | category | flops | bytes accessed | tf_op | source)
XLA Modules:
  0.0 88.0 jit_solution(2816329891569311594)
XLA Ops:
  0.0 2.2 %copy.8 = bf16[8,64,512]{2,0,1:T(8,128)(2,1)} copy(bf16[8,64,512]{2,1,0:T(8,128)(2,1)} %param.2) | data formatting | bytes 1048576 | tf_op args[0]
  2.2 11.2 %copy.7 = bf16[32,64,2048]{2,0,1:T(8,128)(2,1)} copy(bf16[32,64,2048]{2,1,0:T(8,128)(2,1)} %chol.1) | data formatting | bytes 16777216 | tf_op args[1]
  13.4 73.2 %shard_map.28 = f32[4,16,32]{2,1,0:T(8,128)} custom-call(bf16[64,8,512]{2,1,0:T(8,128)(2,1)} %bitcast.8, bf16[64,32,2048]{2,1,0:T(8,128)(2,1)} %bitcast.7, bf16[32,64,2048]{2,1,0:T(8,128)(2,1)} %chol.1), custom_call_target="tpu_custom_call" | custom-call | tf_op jit(solution)/shard_map/pallas_call | solution.py:314
  86.6 1.4 %copy.10 = f32[32,4,16]{0,2,1:T(8,128)} copy(f32[32,4,16]{0,2,1:T(8,128)} %bitcast.9) | data formatting | bytes 16384

commit v2 on v1

--- a/solution.py
+++ b/solution.py
@@ -13,16 +13,16 @@
 ROW_CHUNK = 1024
 X_OF_PIECE = (0, 1, 0, 3)
 ROW_PLAN = (
-    ((0, (1, 0)), (2, (1, 0)), (1, (0,)), (3, (1,))),
-    ((1, (0, 1)), (0, (1,)), (2, ()), (3, ())),
-    ((0, ()), (1, ()), (2, ()), (3, ())),
-    ((3, (1, 0)), (2, (0,)), (0, ()), (1, ())),
+    (((0, (1, 0)), (2, (1, 0))), ((1, (0,)), (3, (1,)))),
+    (((1, (0, 1)),), ((0, (1,)), (2, ()), (3, ()))),
+    ((), ((1, ()), (3, ()), (0, ()), (2, ()))),
+    (((3, (1, 0)),), ((2, (0,)), (0, ()), (1, ()))),
 )
 
 
 def kernel(
-    amp, chol_t, chol, out,
-    rows_l, win, amps, ints, total, turned, parts,
+    amp, chol, out,
+    raw_l, raw_t, out_t, rows_l, win, amps, ints, total, turned, parts,
     loc_sem, t_sem, w_sem, p_sem, l_sem, r_sem, s_sem,
 ):
     g, p = lax.axis_index("grp"), lax.axis_index("pair")
@@ -83,10 +83,25 @@
 
     half = pl.ds(pl.multiple_of(h * 256, 256), 256)
     other = pl.ds(pl.multiple_of((1 - h) * 256, 256), 256)
-    own_t = pltpu.make_async_copy(amp.at[:, :, half], blk(p), loc_sem.at[0])
+
+    def turn(i):
+        own_l[i].wait()
+
+        def body(n, carry):
+            lanes = pl.ds(pl.multiple_of(n * 256, 256), 256)
+            rows_l[h, pl.ds(16 * i, 16), :, lanes] = jnp.swapaxes(raw_l[:, pl.ds(16 * i, 16), lanes], 0, 1)
+            return carry
+
+        lax.fori_loop(0, 8, body, 0)
+
+    own_t = pltpu.make_async_copy(amp, raw_t, loc_sem.at[4])
     own_t.start()
-    own_l = pltpu.make_async_copy(chol_t, rows_l.at[h], loc_sem.at[1])
-    own_l.start()
+    own_l = [
+        pltpu.make_async_copy(chol.at[:, pl.ds(16 * i, 16)], raw_l.at[:, pl.ds(16 * i, 16)], loc_sem.at[i])
+        for i in range(4)
+    ]
+    for c in own_l:
+        c.start()
 
     barrier = pltpu.get_barrier_semaphore()
 
@@ -99,27 +114,31 @@
         i = (me + o) % 16
         return i // 2, (p // 2) * 2 + i % 2, i
 
-    for to in (right, left, lo, hi):
+    for to in (sib, right, left, lo, hi, up, down):
         hello(to)
-    for o in range(1, 16):
-        hello(peer(o)[:2])
     is_source = p == 0
 
     @pl.when((x != 2) & jnp.logical_not(is_source & (g < 4)))
     def _():
         hello((h * 4 + z, 0))
 
+    own_t.wait()
+    amps[p] = jnp.swapaxes(raw_t[:, :, half], 0, 1)
+    out_t[...] = jnp.swapaxes(raw_t[:, :, other], 0, 1)
+    turn(0)
+    turn(1)
+
     @pl.when(jnp.logical_not(is_source))
     def _():
-        pl.semaphore_wait(barrier, 19)
+        pl.semaphore_wait(barrier, 7)
 
     @pl.when(is_source & (y_hi == 0))
     def _():
-        pl.semaphore_wait(barrier, 30)
+        pl.semaphore_wait(barrier, 18)
 
     @pl.when(is_source & (y_hi == 1))
     def _():
-        pl.semaphore_wait(barrier, 31)
+        pl.semaphore_wait(barrier, 19)
 
     n_scatter = n_sent[0]
 
@@ -143,48 +162,66 @@
 
     n_sent[0] = n_scatter + 16
 
-    send(amp.at[:, :, other], blk(p), t_sem.at[p], sib)
-    own_t.wait()
-    for to in (right, left, lo):
-        send_t(p, to)
-    send(chol_t, rows_l.at[h], l_sem, sib)
-
-    n_row = n_sent[0]
+    send(out_t, blk(p), t_sem.at[p], sib)
+
+    def send_t_part(d, n, to):
+        send(blk(p).at[pl.ds(d, n)], blk(p).at[pl.ds(d, n)], t_sem.at[p], to)
+
+    send_t_part(0, 16, right)
+    send_t_part(0, 16, left)
+    send_t(p, lo)
+    turn(2)
+    turn(3)
+    send(rows_l.at[h], rows_l.at[h], l_sem, sib)
 
     def got(j):
         arrived(piece(y, z, j), p_sem.at[j])
 
-    def row(xx):
-        k = n_row
-        for j, tos in ROW_PLAN[xx]:
+    def row(xx, part, k):
+        for j, tos in ROW_PLAN[xx][part]:
+            quarter = piece(y, z, j)
             copies = []
-            for to in tos:
-                copies.append(remote(piece(y, z, j), piece(y, z, j), p_sem.at[j], (left, right)[to], k))
+            for recv, to in [(p_sem.at[j], (left, right)[t]) for t in tos] + [
+                (w_sem.at[y * 4 + z], to) for to in (down, up, hi, lo)
+            ]:
+                copies.append(remote(quarter, quarter, recv, to, k))
                 k += 1
             yield j, copies
 
-    for xx in range(4):
-
-        @pl.when(x == xx)
-        def _():
-            for j, copies in row(xx):
-                got(j)
-                for c in copies:
-                    c.start()
-
-    n_sent[0] = n_row + 6
-
-    for to in (down, up, hi, lo):
-        send_w(y, z, to)
-    sib_p = (p // 2) * 2 + (1 - h)
+    n_row = []
+    for part in (0, 1):
+        n_row.append(n_sent[0])
+        for xx in range(4):
+            if ROW_PLAN[xx][part]:
+
+                @pl.when(x == xx)
+                def _():
+                    for j, copies in row(xx, part, n_row[part]):
+                        got(j)
+                        for c in copies:
+                            c.start()
+
+        n_sent[0] += 18
+        if part == 0:
+            send_t_part(16, 16, right)
+            send_t_part(16, 16, left)
+    send_t_part(32, 32, right)
+    send_t_part(32, 32, left)
+
+    mine = x * 4 + y_lo * 2
+    sib_p = mine + (1 - h)
+    lo_p = x * 4 + (1 - y_lo) * 2 + h
+    lo_s = x * 4 + (1 - y_lo) * 2 + (1 - h)
+    fr = xl * 4 + y_lo * 2
+    gr = xr * 4 + y_lo * 2
+    fl = xr * 4 + (1 - y_lo) * 2
+    gl = xl * 4 + (1 - y_lo) * 2
     wait_t(sib_p)
     for to in (right, left, lo):
         send_t(sib_p, to)
     wait_w(y_l, z)
     for to in (down, up, hi):
         send_w(y_l, z, to)
-    lo_p = x * 4 + (1 - y_lo) * 2 + h
-    lo_s = x * 4 + (1 - y_lo) * 2 + (1 - h)
     wait_t(lo_p)
     for to in (right, left):
         send_t(lo_p, to)
@@ -193,26 +230,12 @@
     wait_w(y, zu)
     send_w(y, zu, hi)
     send_w(y, zu, down)
-    wait_w(y_f, z)
-    for to in (down, up):
-        send_w(y_f, z, to)
-    fr = xl * 4 + y_lo * 2
-    fl = xr * 4 + (1 - y_lo) * 2
     wait_t(fr + h)
     send_t(fr + h, right)
-    wait_t(lo_s)
-    for to in (right, left):
-        send_t(lo_s, to)
-    wait_t(fl + h)
-    send_t(fl + h, left)
-    wait_t(fr + (1 - h))
-    send_t(fr + (1 - h), right)
-
     wait_w(y_l, zd)
     send_w(y_l, zd, up)
     wait_w(y_l, zu)
 
-    own_l.wait()
     arrived(rows_l.at[1 - h], l_sem)
 
     wide = ROW_CHUNK // 32
@@ -231,31 +254,43 @@
                 )
             return carry
 
-        lax.fori_loop(0, 2 * (64 // wide), body, 0)
+        lax.fori_loop(0, 2 * (64 // wide), body, 0, unroll=True)
 
     zz, aa = z // 2, y // 2
     tile(zz, aa)
 
+    wait_w(y_f, z)
+    for to in (down, up):
+        send_w(y_f, z, to)
+    wait_t(fr + (1 - h))
+    send_t(fr + (1 - h), lo)
+    send_t(fr + (1 - h), right)
+    wait_t(gr + (1 - h))
+    send_t(gr + (1 - h), lo)
+    wait_t(fl + h)
+    send_t(fl + h, left)
+    wait_w(y_h, zd)
+    send_w(y_h, zd, up)
+    wait_w(y, zf)
+    wait_w(y_l, zf)
+    tile(1 - zz, aa)
+
+    wait_w(y_f, zu)
+    send_w(y_f, zu, down)
     wait_t(fl + (1 - h))
     send_t(fl + (1 - h), left)
-    wait_w(y_h, zd)
-    send_w(y_h, zd, up)
-    wait_w(y_f, zu)
-    send_w(y_f, zu, down)
     wait_w(y_h, zu)
     wait_w(y_h, z)
     wait_w(y_f, zd)
     tile(zz, 1 - aa)
-    wait_w(y, zf)
-    wait_w(y_l, zf)
-    tile(1 - zz, aa)
     wait_w(y_f, zf)
     wait_w(y_h, zf)
     tile(1 - zz, 1 - aa)
 
+    wait_t(lo_s)
+    wait_t(gr + h)
     for k in (0, 1):
-        wait_t(xr * 4 + y_lo * 2 + k)
-        wait_t(xl * 4 + (1 - y_lo) * 2 + k)
+        wait_t(gl + k)
     for k in range(4):
         wait_t(((x + 2) % 4) * 4 + k)
 
@@ -263,8 +298,8 @@
 
     def step(i, carry):
         acc = None
-        for u in range(4):
-            d = i * 4 + u
+        for u in range(16):
+            d = i * 16 + u
             o = lax.dot_general(
                 ints[d].reshape(256, 256), amps[:, d].reshape(128, 256), (((1,), (1,)), ((), ())),
                 preferred_element_type=F32,
@@ -273,8 +308,29 @@
         total[...] += acc
         return carry
 
-    lax.fori_loop(0, 16, step, 0)
+    lax.fori_loop(0, 4, step, 0)
     turned[...] = total[...].T
+
+    for c in started:
+        c.wait_send()
+    started.clear()
+    for top in (0, 1):
+
+        @pl.when(is_source & (y_hi == top))
+        def _():
+            for away, _ in scatter(top):
+                if away is not None:
+                    away.wait_send()
+
+    for part in (0, 1):
+        for xx in range(4):
+            if ROW_PLAN[xx][part]:
+
+                @pl.when(x == xx)
+                def _():
+                    for _, copies in row(xx, part, n_row[part]):
+                        for c in copies:
+                            c.wait_send()
 
     for o in range(1, 16):
         gg, pp, i = peer(o)
@@ -292,21 +348,6 @@
 
     for c in started:
         c.wait_send()
-    for top in (0, 1):
-
-        @pl.when(is_source & (y_hi == top))
-        def _():
-            for away, _ in scatter(top):
-                if away is not None:
-                    away.wait_send()
-
-    for xx in (0, 1, 3):
-
-        @pl.when(x == xx)
-        def _():
-            for _, copies in row(xx):
-                for c in copies:
-                    c.wait_send()
 
 
 def per_device(amplitudes, cholesky):
@@ -314,9 +355,12 @@
     out = pl.pallas_call(
         kernel,
         out_shape=jax.ShapeDtypeStruct((A_WIN, 16, 32), F32),
-        in_specs=[hbm] * 3,
+        in_specs=[hbm] * 2,
         out_specs=pl.BlockSpec(memory_space=pltpu.VMEM),
         scratch_shapes=[
+            pltpu.VMEM((32, 64, 2048), BF16),
+            pltpu.VMEM((8, 64, 512), BF16),
+            pltpu.VMEM((64, 8, 256), BF16),
             pltpu.VMEM((2, 64, 32, 2048), BF16),
             pltpu.VMEM((2, A_WIN, 2, 64, 2048), BF16),
             pltpu.VMEM((16, 64, 8, 256), BF16),
@@ -324,18 +368,18 @@
             pltpu.VMEM((256, 128), F32),
             pltpu.VMEM((128, 256), F32),
             pltpu.VMEM((16, 16, 128), F32),
-            pltpu.SemaphoreType.DMA((2,)),
+            pltpu.SemaphoreType.DMA((5,)),
             pltpu.SemaphoreType.DMA((16,)),
             pltpu.SemaphoreType.DMA((16,)),
             pltpu.SemaphoreType.DMA((4,)),
             pltpu.SemaphoreType.DMA,
             pltpu.SemaphoreType.DMA((16,)),
-            pltpu.SemaphoreType.DMA((80,)),
+            pltpu.SemaphoreType.DMA((112,)),
         ],
         compiler_params=pltpu.CompilerParams(
             collective_id=0, has_side_effects=True, vmem_limit_bytes=56 * 2**20
         ),
-    )(amplitudes.transpose(1, 0, 2), cholesky.transpose(1, 0, 2), cholesky)
+    )(amplitudes, cholesky)
     return out.transpose(2, 0, 1)
 
 

time: 89.3 us -> 69.5 us (0.78)
  the two profiles are of different devices: /device:TPU:5 before, /device:TPU:3 now
where the time goes in v2:
time: 69.5 us; the launch traced here: 69.3 us
  Pallas kernels  68 us (98%)
  local copies, waits for them, and re-layouts  1.38 us (2%)
    pallas_call x1, Pallas kernels, per_device(): pl.pallas_call(kernel, out_shape=jax.ShapeDtypeStruct((A_WIN, 16, 32), F3...  68 us

profile of v2, /device:TPU:3, one launch (start us, length us, event | category | flops | bytes accessed | tf_op | source)
XLA Modules:
  0.0 69.3 jit_solution(2936599942412465087)
XLA Ops:
  0.0 68.0 %shard_map.28 = f32[4,16,32]{2,1,0:T(8,128)} custom-call(bf16[8,64,512]{2,1,0:T(8,128)(2,1)} %amp.1, bf16[32,64,2048]{2,1,0:T(8,128)(2,1)} %chol.1), custom_call_target="tpu_custom_call" | custom-call | tf_op jit(solution)/shard_map/pallas_call | solution.py:355
  68.0 1.4 %copy.4 = f32[32,4,16]{0,2,1:T(8,128)} copy(f32[32,4,16]{0,2,1:T(8,128)} %bitcast.1) | data formatting | bytes 16384

commit v3 on v2

--- a/solution.py
+++ b/solution.py
@@ -11,19 +11,19 @@
 
 
 ROW_CHUNK = 1024
-X_OF_PIECE = (0, 1, 0, 3)
+ENTRIES = (((0, 0), (0, 2), (1, 1), (3, 3)), ((0, 1), (0, 3)))
 ROW_PLAN = (
-    (((0, (1, 0)), (2, (1, 0))), ((1, (0,)), (3, (1,)))),
-    (((1, (0, 1)),), ((0, (1,)), (2, ()), (3, ()))),
-    ((), ((1, ()), (3, ()), (0, ()), (2, ()))),
-    (((3, (1, 0)),), ((2, (0,)), (0, ()), (1, ()))),
+    ((0, (1, 0)), (2, (1, 0)), (1, (0,)), (3, (1,))),
+    ((1, (1,)), (0, (1,)), (2, ()), (3, ())),
+    ((1, ()), (3, ()), (0, ()), (2, ())),
+    ((3, (0,)), (2, (0,)), (0, ()), (1, ())),
 )
 
 
 def kernel(
     amp, chol, out,
     raw_l, raw_t, out_t, rows_l, win, amps, ints, total, turned, parts,
-    loc_sem, t_sem, w_sem, p_sem, l_sem, r_sem, s_sem,
+    loc_sem, t_sem, w_sem, p_sem, q_sem, u_sem, v_sem, l_sem, r_sem, s_sem,
 ):
     g, p = lax.axis_index("grp"), lax.axis_index("pair")
     x, y_lo, h = p // 4, (p // 2) % 2, p % 2
@@ -144,14 +144,15 @@
 
     def scatter(top):
         k = n_scatter
-        for qy in ((2 * top + 2) % 4, (2 * top + 1) % 4, (2 * top + 3) % 4, 2 * top):
-            for j in (1, 3, 0, 2):
-                src, dst = chol.at[qy, pl.ds(16 * j, 16)], piece(qy, z, j)
-                if top == 0 and qy == 0 and X_OF_PIECE[j] == 0:
-                    yield None, pltpu.make_async_copy(src, dst, p_sem.at[j])
-                else:
-                    yield remote(src, dst, p_sem.at[j], dev(X_OF_PIECE[j], qy, z, top), k), None
-                    k += 1
+        for entries in ENTRIES:
+            for qy in ((2 * top + 2) % 4, (2 * top + 1) % 4, (2 * top + 3) % 4, 2 * top):
+                for to_x, j in entries:
+                    src, dst = chol.at[qy, pl.ds(16 * j, 16)], piece(qy, z, j)
+                    if top == 0 and qy == 0 and to_x == 0:
+                        yield None, pltpu.make_async_copy(src, dst, p_sem.at[j])
+                    else:
+                        yield remote(src, dst, p_sem.at[j], dev(to_x, qy, z, top), k), None
+                        k += 1
 
     for top in (0, 1):
 
@@ -160,7 +161,7 @@
             for away, here in scatter(top):
                 (away or here).start()
 
-    n_sent[0] = n_scatter + 16
+    n_sent[0] = n_scatter + 24
 
     send(out_t, blk(p), t_sem.at[p], sib)
 
@@ -169,7 +170,6 @@
 
     send_t_part(0, 16, right)
     send_t_part(0, 16, left)
-    send_t(p, lo)
     turn(2)
     turn(3)
     send(rows_l.at[h], rows_l.at[h], l_sem, sib)
@@ -177,37 +177,44 @@
     def got(j):
         arrived(piece(y, z, j), p_sem.at[j])
 
-    def row(xx, part, k):
-        for j, tos in ROW_PLAN[xx][part]:
+    def row(xx, k):
+        for j, tos in ROW_PLAN[xx]:
             quarter = piece(y, z, j)
             copies = []
             for recv, to in [(p_sem.at[j], (left, right)[t]) for t in tos] + [
-                (w_sem.at[y * 4 + z], to) for to in (down, up, hi, lo)
+                (w_sem.at[y * 4 + z], down), (w_sem.at[y * 4 + z], up), (q_sem.at[j], lo), (w_sem.at[y * 4 + z], hi)
             ]:
                 copies.append(remote(quarter, quarter, recv, to, k))
                 k += 1
             yield j, copies
 
-    n_row = []
-    for part in (0, 1):
-        n_row.append(n_sent[0])
-        for xx in range(4):
-            if ROW_PLAN[xx][part]:
-
-                @pl.when(x == xx)
-                def _():
-                    for j, copies in row(xx, part, n_row[part]):
-                        got(j)
-                        for c in copies:
-                            c.start()
-
-        n_sent[0] += 18
-        if part == 0:
-            send_t_part(16, 16, right)
-            send_t_part(16, 16, left)
-    send_t_part(32, 32, right)
-    send_t_part(32, 32, left)
-
+    def row_l(xx, k):
+        for j, _ in ROW_PLAN[xx]:
+            quarter = piece(y_l, z, j)
+            block = w_sem.at[y_l * 4 + z]
+            yield j, [
+                remote(quarter, quarter, recv, to, k + n)
+                for n, (recv, to) in enumerate(((block, down), (u_sem.at[j], up), (block, hi)))
+            ]
+            k += 3
+
+    def row_u(xx, k):
+        for j, _ in ROW_PLAN[xx]:
+            quarter = piece(y_l, zd, j)
+            yield j, [remote(quarter, quarter, w_sem.at[y_l * 4 + zd], up, k)]
+            k += 1
+
+    n_row = n_sent[0]
+    for xx in range(4):
+
+        @pl.when(x == xx)
+        def _():
+            for j, copies in row(xx, n_row):
+                got(j)
+                for c in copies:
+                    c.start()
+
+    n_sent[0] += 22
     mine = x * 4 + y_lo * 2
     sib_p = mine + (1 - h)
     lo_p = x * 4 + (1 - y_lo) * 2 + h
@@ -217,69 +224,96 @@
     fl = xr * 4 + (1 - y_lo) * 2
     gl = xl * 4 + (1 - y_lo) * 2
     wait_t(sib_p)
-    for to in (right, left, lo):
+    for to in (right, left):
         send_t(sib_p, to)
-    wait_w(y_l, z)
-    for to in (down, up, hi):
-        send_w(y_l, z, to)
-    wait_t(lo_p)
     for to in (right, left):
-        send_t(lo_p, to)
+        send_t_part(16, 48, to)
+    send_t(p, lo)
+    send_t(sib_p, lo)
+    n_row_l = n_sent[0]
+    for xx in range(4):
+
+        @pl.when(x == xx)
+        def _():
+            for j, copies in row_l(xx, n_row_l):
+                arrived(piece(y_l, z, j), q_sem.at[j])
+                for c in copies:
+                    c.start()
+
+    n_sent[0] += 12
     wait_w(y, zd)
     send_w(y, zd, hi)
     wait_w(y, zu)
     send_w(y, zu, hi)
     send_w(y, zu, down)
-    wait_t(fr + h)
-    send_t(fr + h, right)
-    wait_w(y_l, zd)
-    send_w(y_l, zd, up)
+    n_row_u = n_sent[0]
+    for xx in range(4):
+
+        @pl.when(x == xx)
+        def _():
+            for j, copies in row_u(xx, n_row_u):
+                arrived(piece(y_l, zd, j), u_sem.at[j])
+                for c in copies:
+                    c.start()
+
+    n_sent[0] += 4
     wait_w(y_l, zu)
-
     arrived(rows_l.at[1 - h], l_sem)
 
     wide = ROW_CHUNK // 32
 
-    def tile(zz, aa):
+    def tile(zz, aa, halves=(0, 1)):
         w = win[zz, pl.ds(2 * aa, 2)].reshape(256, 2048)
         lanes = pl.ds(pl.multiple_of(zz * 128, 128), 128)
-
-        def body(i, carry):
-            k, d0 = i // (64 // wide), (i % (64 // wide)) * wide
-            l = rows_l[k, pl.ds(d0, wide)].reshape(ROW_CHUNK, 2048)
-            o = lax.dot_general(l, w, (((1,), (1,)), ((), ())), preferred_element_type=F32).astype(BF16)
-            for q in (0, 1):
-                ints[pl.ds(d0, wide), k * 4 + 2 * aa + q, :, lanes] = o[:, q * 128 : q * 128 + 128].reshape(
-                    wide, 32, 128
-                )
-            return carry
-
-        lax.fori_loop(0, 2 * (64 // wide), body, 0, unroll=True)
+        for k in halves:
+            for d0 in range(0, 64, wide):
+                l = rows_l[k, pl.ds(d0, wide)].reshape(ROW_CHUNK, 2048)
+                o = lax.dot_general(l, w, (((1,), (1,)), ((), ())), preferred_element_type=F32).astype(BF16)
+                for q in (0, 1):
+                    ints[pl.ds(d0, wide), k * 4 + 2 * aa + q, :, lanes] = o[:, q * 128 : q * 128 + 128].reshape(
+                        wide, 32, 128
+                    )
 
     zz, aa = z // 2, y // 2
-    tile(zz, aa)
-
+    tile(zz, aa, (0,))
     wait_w(y_f, z)
-    for to in (down, up):
-        send_w(y_f, z, to)
+    for q in (0, 1):
+        half_w = wblk(y_f, z).at[pl.ds(32 * q, 32)]
+        send(half_w, half_w, v_sem.at[q], down)
+    send_w(y_f, z, up)
     wait_t(fr + (1 - h))
     send_t(fr + (1 - h), lo)
     send_t(fr + (1 - h), right)
     wait_t(gr + (1 - h))
     send_t(gr + (1 - h), lo)
+    wait_t(lo_p)
+    for to in (right, left):
+        send_t(lo_p, to)
+    tile(zz, aa, (1,))
+
+    wait_t(fr + h)
+    send_t(fr + h, right)
+    wait_w(y, zf)
+    send_w(y, zf, hi)
+    wait_w(y_l, zf)
+
+    def forward_f(q):
+        half_w = wblk(y_f, zu).at[pl.ds(32 * q, 32)]
+        arrived(half_w, v_sem.at[q])
+        send(half_w, half_w, w_sem.at[y_f * 4 + zu], down)
+
+    tile(1 - zz, aa, (0,))
+    forward_f(0)
+    tile(1 - zz, aa, (1,))
+    forward_f(1)
     wait_t(fl + h)
     send_t(fl + h, left)
+    away = ((x + 2) % 4) * 4
+    wait_t(away + y_lo * 2 + (1 - h))
+    send_t(away + y_lo * 2 + (1 - h), lo)
+
+    wait_w(y_h, zu)
     wait_w(y_h, zd)
-    send_w(y_h, zd, up)
-    wait_w(y, zf)
-    wait_w(y_l, zf)
-    tile(1 - zz, aa)
-
-    wait_w(y_f, zu)
-    send_w(y_f, zu, down)
-    wait_t(fl + (1 - h))
-    send_t(fl + (1 - h), left)
-    wait_w(y_h, zu)
     wait_w(y_h, z)
     wait_w(y_f, zd)
     tile(zz, 1 - aa)
@@ -291,8 +325,10 @@
     wait_t(gr + h)
     for k in (0, 1):
         wait_t(gl + k)
-    for k in range(4):
-        wait_t(((x + 2) % 4) * 4 + k)
+    wait_t(fl + (1 - h))
+    wait_t(away + y_lo * 2 + h)
+    for k in (0, 1):
+        wait_t(away + (1 - y_lo) * 2 + k)
 
     total[...] = jnp.zeros_like(total)
 
@@ -322,15 +358,13 @@
                 if away is not None:
                     away.wait_send()
 
-    for part in (0, 1):
-        for xx in range(4):
-            if ROW_PLAN[xx][part]:
-
-                @pl.when(x == xx)
-                def _():
-                    for _, copies in row(xx, part, n_row[part]):
-                        for c in copies:
-                            c.wait_send()
+    for xx in range(4):
+
+        @pl.when(x == xx)
+        def _():
+            for _, copies in (*row(xx, n_row), *row_l(xx, n_row_l), *row_u(xx, n_row_u)):
+                for c in copies:
+                    c.wait_send()
 
     for o in range(1, 16):
         gg, pp, i = peer(o)
@@ -372,9 +406,12 @@
             pltpu.SemaphoreType.DMA((16,)),
             pltpu.SemaphoreType.DMA((16,)),
             pltpu.SemaphoreType.DMA((4,)),
+            pltpu.SemaphoreType.DMA((4,)),
+            pltpu.SemaphoreType.DMA((4,)),
+            pltpu.SemaphoreType.DMA((2,)),
             pltpu.SemaphoreType.DMA,
             pltpu.SemaphoreType.DMA((16,)),
-            pltpu.SemaphoreType.DMA((112,)),
+            pltpu.SemaphoreType.DMA((128,)),
         ],
         compiler_params=pltpu.CompilerParams(
             collective_id=0, has_side_effects=True, vmem_limit_bytes=56 * 2**20

time: 69.5 us -> 64.4 us (0.927)
  the two profiles are of different devices: /device:TPU:3 before, /device:TPU:5 now
where the time goes in v3:
time: 64.4 us; the launch traced here: 64.3 us
  Pallas kernels  62.9 us (98%)
  local copies, waits for them, and re-layouts  1.38 us (2%)
    pallas_call x1, Pallas kernels, per_device(): pl.pallas_call(kernel, out_shape=jax.ShapeDtypeStruct((A_WIN, 16, 32), F3...  62.9 us
    unnamed x1, local copies, waits for them, and re-layouts  1.38 us

profile of v3, /device:TPU:5, one launch (start us, length us, event | category | flops | bytes accessed | tf_op | source)
XLA Modules:
  0.0 64.3 jit_solution(16484038233817412306)
XLA Ops:
  0.0 62.9 %shard_map.28 = f32[4,16,32]{2,1,0:T(8,128)} custom-call(bf16[8,64,512]{2,1,0:T(8,128)(2,1)} %amp.1, bf16[32,64,2048]{2,1,0:T(8,128)(2,1)} %chol.1), custom_call_target="tpu_custom_call" | custom-call | tf_op jit(solution)/shard_map/pallas_call | solution.py:389
  62.9 1.4 %copy.4 = f32[32,4,16]{0,2,1:T(8,128)} copy(f32[32,4,16]{0,2,1:T(8,128)} %bitcast.1) | data formatting | bytes 16384

commit v4 on v3

--- a/solution.py
+++ b/solution.py
@@ -11,6 +11,7 @@
 
 
 ROW_CHUNK = 1024
+PEERS = tuple((dy, dz, dk) for dy in (1, 0) for dz in (2, 1, 3, 0) for dk in (1, 0))[:15]
 ENTRIES = (((0, 0), (0, 2), (1, 1), (3, 3)), ((0, 1), (0, 3)))
 ROW_PLAN = (
     ((0, (1, 0)), (2, (1, 0)), (1, (0,)), (3, (1,))),
@@ -111,8 +112,9 @@
     me = g * 2 + h
 
     def peer(o):
-        i = (me + o) % 16
-        return i // 2, (p // 2) * 2 + i % 2, i
+        dy, dz, dk = PEERS[o - 1]
+        gg, k = ((y_hi + dy) % 2) * 4 + (z + dz) % 4, (h + dk) % 2
+        return gg, (p // 2) * 2 + k, gg * 2 + k
 
     for to in (sib, right, left, lo, hi, up, down):
         hello(to)
@@ -125,8 +127,6 @@
     own_t.wait()
     amps[p] = jnp.swapaxes(raw_t[:, :, half], 0, 1)
     out_t[...] = jnp.swapaxes(raw_t[:, :, other], 0, 1)
-    turn(0)
-    turn(1)
 
     @pl.when(jnp.logical_not(is_source))
     def _():
@@ -170,8 +170,8 @@
 
     send_t_part(0, 16, right)
     send_t_part(0, 16, left)
-    turn(2)
-    turn(3)
+    for i in range(4):
+        turn(i)
     send(rows_l.at[h], rows_l.at[h], l_sem, sib)
 
     def got(j):
@@ -241,11 +241,13 @@
                     c.start()
 
     n_sent[0] += 12
+    z_pair = z + 1 - 2 * (z % 2)
+    z_other = (2 * z - z_pair + 4) % 4
     wait_w(y, zd)
-    send_w(y, zd, hi)
     wait_w(y, zu)
-    send_w(y, zu, hi)
     send_w(y, zu, down)
+    send_w(y, z_pair, hi)
+    send_w(y, z_other, hi)
     n_row_u = n_sent[0]
     for xx in range(4):
 
@@ -312,11 +314,11 @@
     wait_t(away + y_lo * 2 + (1 - h))
     send_t(away + y_lo * 2 + (1 - h), lo)
 
-    wait_w(y_h, zu)
-    wait_w(y_h, zd)
     wait_w(y_h, z)
+    wait_w(y_h, z_pair)
     wait_w(y_f, zd)
     tile(zz, 1 - aa)
+    wait_w(y_h, z_other)
     wait_w(y_f, zf)
     wait_w(y_h, zf)
     tile(1 - zz, 1 - aa)
@@ -373,7 +375,7 @@
             parts.at[me], r_sem.at[me], (gg, pp),
         )
     acc = turned[pl.ds(pl.multiple_of(g * 16, 16), 16), pl.ds(pl.multiple_of(h * 128, 128), 128)]
-    for o in range(1, 16):
+    for o in range(15, 0, -1):
         i = peer(o)[2]
         arrived(parts.at[i], r_sem.at[i])
         acc = acc + parts[i]

time: 64.4 us -> 64 us (level)
  no operation moved by 1% of the time
where the time goes in v4:
time: 64 us; the launch traced here: 63.8 us
  Pallas kernels  62.4 us (98%)
  local copies, waits for them, and re-layouts  1.38 us (2%)
    pallas_call x1, Pallas kernels, per_device(): pl.pallas_call(kernel, out_shape=jax.ShapeDtypeStruct((A_WIN, 16, 32), F3...  62.4 us
    unnamed x1, local copies, waits for them, and re-layouts  1.38 us

profile of v4, /device:TPU:5, one launch (start us, length us, event | category | flops | bytes accessed | tf_op | source)
XLA Modules:
  0.0 63.8 jit_solution(8994375346683109766)
XLA Ops:
  0.0 62.4 %shard_map.28 = f32[4,16,32]{2,1,0:T(8,128)} custom-call(bf16[8,64,512]{2,1,0:T(8,128)(2,1)} %amp.1, bf16[32,64,2048]{2,1,0:T(8,128)(2,1)} %chol.1), custom_call_target="tpu_custom_call" | custom-call | tf_op jit(solution)/shard_map/pallas_call | solution.py:391
  62.4 1.4 %copy.4 = f32[32,4,16]{0,2,1:T(8,128)} copy(f32[32,4,16]{0,2,1:T(8,128)} %bitcast.1) | data formatting | bytes 16384

commit v5 on v4

--- a/solution.py
+++ b/solution.py
@@ -310,14 +310,15 @@
     forward_f(1)
     wait_t(fl + h)
     send_t(fl + h, left)
+
+    wait_w(y_h, z)
+    wait_w(y_h, z_pair)
+    wait_w(y_f, zd)
+    tile(zz, 1 - aa, (0,))
     away = ((x + 2) % 4) * 4
     wait_t(away + y_lo * 2 + (1 - h))
     send_t(away + y_lo * 2 + (1 - h), lo)
-
-    wait_w(y_h, z)
-    wait_w(y_h, z_pair)
-    wait_w(y_f, zd)
-    tile(zz, 1 - aa)
+    tile(zz, 1 - aa, (1,))
     wait_w(y_h, z_other)
     wait_w(y_f, zf)
     wait_w(y_h, zf)

time: 64 us -> 64.2 us (level)
  no operation moved by 1% of the time
where the time goes in v5:
time: 64.2 us; the launch traced here: 64 us
  Pallas kernels  62.6 us (98%)
  local copies, waits for them, and re-layouts  1.38 us (2%)
    pallas_call x1, Pallas kernels, per_device(): pl.pallas_call(kernel, out_shape=jax.ShapeDtypeStruct((A_WIN, 16, 32), F3...  62.6 us
    unnamed x1, local copies, waits for them, and re-layouts  1.38 us

profile of v5, /device:TPU:5, one launch (start us, length us, event | category | flops | bytes accessed | tf_op | source)
XLA Modules:
  0.0 64.0 jit_solution(16044592019575360036)
XLA Ops:
  0.0 62.6 %shard_map.28 = f32[4,16,32]{2,1,0:T(8,128)} custom-call(bf16[8,64,512]{2,1,0:T(8,128)(2,1)} %amp.1, bf16[32,64,2048]{2,1,0:T(8,128)(2,1)} %chol.1), custom_call_target="tpu_custom_call" | custom-call | tf_op jit(solution)/shard_map/pallas_call | solution.py:392
  62.6 1.4 %copy.4 = f32[32,4,16]{0,2,1:T(8,128)} copy(f32[32,4,16]{0,2,1:T(8,128)} %bitcast.1) | data formatting | bytes 16384
